TPU v7x, 8 devices: a whole 2x2x1 slice. The times are simulated.
8 devices in a mesh: dp: 2 (over z, y), sp: 4 (over x, core).
Axes of the slice: x: 2, y: 2, z: 1, core: 2. Of those that a mesh axis runs over, the one named last changes fastest.
Arguments:
- feature_map: bfloat16 [400, 336, 256], P(('dp', 'sp')), parts along dimension 0
- box_coords: int32 [2048, 4], P('dp'), parts along dimension 0
- w_one: bfloat16 [12544, 1024], replicated
- b_one: float32 [1024], replicated
- w_two: bfloat16 [1024, 1024], replicated
- b_two: float32 [1024], replicated
Outputs:
- output: bfloat16 [2048, 1024], P(('dp', 'sp')), parts along dimension 0
There are 2 independent parts. A program takes and returns all parts, laid end to end along the dimension named above; an argument that names none is the same for every part.
All inputs are finite; a program needn't handle non-finite values.
Results may differ from a plain program's by a relative error of at most 0.00712392.
Values are sent between devices in bfloat16 or wider.
A program may use at most 1 GiB of HBM per device.

v0:
```python
import jax
import jax.numpy as jnp
from jax import lax
from jax.sharding import PartitionSpec as P

POOL_BINS = 7


def bin_weights(start_eighths, span_units, length, offset, num_rows):
    sample_ids = jnp.arange(2 * POOL_BINS, dtype=jnp.int32)
    sample_pos = 4 * start_eighths[..., None] - 16 + (2 * sample_ids + 1) * span_units[..., None]
    inside = (sample_pos >= -32) & (sample_pos <= 32 * length)
    sample_pos = jnp.maximum(sample_pos, 0)
    low_row = sample_pos // 32
    frac_part = sample_pos % 32
    at_top = low_row >= length - 1
    low_row = jnp.where(at_top, length - 1, low_row)
    frac_part = jnp.where(at_top, 0, frac_part)
    low_wt = jnp.where(inside, 32 - frac_part, 0)
    high_wt = jnp.where(inside, frac_part, 0)
    grid_rows = offset + jnp.arange(num_rows, dtype=jnp.int32)
    weights = (grid_rows == low_row[..., None]) * low_wt[..., None] + (grid_rows == low_row[..., None] + 1) * high_wt[..., None]
    weights = weights.reshape(weights.shape[:-2] + (POOL_BINS, 2, num_rows)).sum(axis=-2)
    return (weights.astype(jnp.float32) / 64.0).astype(jnp.bfloat16)


def box_head(pooled, w_one, b_one, w_two, b_two):
    hidden_act = jnp.maximum(jnp.dot(pooled, w_one, preferred_element_type=jnp.float32) + b_one, 0.0).astype(jnp.bfloat16)
    return jnp.maximum(jnp.dot(hidden_act, w_two, preferred_element_type=jnp.float32) + b_two, 0.0).astype(jnp.bfloat16)


def solution(mesh):
    group_size = mesh.shape['sp']

    def device_step(feature_map, box_coords, w_one, b_one, w_two, b_two):
        tile_rows, feat_w, channels = feature_map.shape
        regions = box_coords.shape[0]
        tile_id = lax.axis_index('sp')
        span_y = (box_coords[:, 2] - box_coords[:, 0]) // 7
        span_x = (box_coords[:, 3] - box_coords[:, 1]) // 7
        row_wts = bin_weights(box_coords[:, 0], span_y, tile_rows * group_size, tile_id * tile_rows, tile_rows)
        col_wts = bin_weights(box_coords[:, 1], span_x, feat_w, 0, feat_w)
        across = jnp.einsum('rjw,hwc->rjhc', col_wts, feature_map, preferred_element_type=jnp.float32)
        tile_part = jnp.einsum('rih,rjhc->rijc', row_wts.astype(jnp.float32), across, precision=lax.Precision.HIGHEST, preferred_element_type=jnp.float32)
        tile_part = tile_part.astype(jnp.bfloat16).reshape(regions, POOL_BINS * POOL_BINS * channels)
        pooled = lax.psum_scatter(tile_part, 'sp', scatter_dimension=0, tiled=True)
        return box_head(pooled, w_one, b_one, w_two, b_two)

    return jax.shard_map(device_step, mesh=mesh, in_specs=(P(('dp', 'sp'), None, None), P('dp', None), P(), P(), P(), P()), out_specs=P(('dp', 'sp'), None), check_vma=False)
```

profile of v0, /device:TPU:0, one launch (start us, length us, event | category | flops | bytes accessed | tf_op | source)
XLA Modules:
  0.0 690.1 jit_solution(3386835722748727021)
XLA Ops:
  6.5 0.0 copy-start
  6.5 0.0 reduce-scatter.2.cloned.1.call-start
  6.6 1.0 multiply_add_fusion.2
  7.5 0.6 compare_select_fusion.3
  8.1 5.5 fusion.11
  13.6 0.2 fusion.16
  13.8 2.7 copy.12
  16.5 9.8 %add_reduce_fusion = s32[1024,7,336]{0,2,1:T(8,128)} fusion(s32[1024,7,2]{0,2,1:T(2,128)S(1)} %get-tuple-element.10, s32[1024,7,2]{0,2,1:T(2,128)S(1)} %get-tuple-element.11, s32[1024,7,2]{0,2,1:T(2,128)S(1)} %get-tuple-element.12, s32[1024,7,2]{0,2,1:T(2,128)S(1)} %get-tuple-element.9), kind=kLoop, calls=%fused_computation.2 | loop fusion | flops 26492928 | bytes 9863168 | tf_op jit(solution)/shard_map/reduce_sum | solution.py:23
  26.3 129.8 %fusion.5 = f32[1024,7,50,256]{3,0,2,1:T(8,128)} fusion(bf16[50,336,256]{2,1,0:T(8,128)(2,1)} %param.6, s32[1024,7,336]{0,2,1:T(8,128)} %add_reduce_fusion), kind=kOutput, calls=%fused_computation.7 | convolution fusion | flops 61663494144 | bytes 385236992 | tf_op jit(solution)/shard_map/rjw,hwc->rjhc/dot_general | solution.py:43
  156.2 297.7 %fusion.2 = bf16[1024,7,7,256]{3,1,2,0:T(8,128)(2,1)} fusion(bf16[1024,7,50,1]{2,1,3,0:T(8,128)(2,1)} %copy.12, f32[1024,7,50,256]{3,0,2,1:T(8,128)} %fusion.5), kind=kOutput, calls=%fused_computation.5 | convolution fusion | flops 7719878656 | bytes 393408512 | tf_op jit(solution)/shard_map/rih,rjhc->rijc/dot_general | solution.py:44
  453.9 38.6 %copy.10 = bf16[1024,7,7,256]{0,3,2,1:T(8,128)(2,1)} copy(bf16[1024,7,7,256]{3,1,2,0:T(8,128)(2,1)} %fusion.2) | data formatting | bytes 51380224 | tf_op jit(solution)/shard_map/convert_element_type | solution.py:45
  492.5 0.0 copy-start.1
  492.5 0.0 copy-start.2
  492.5 0.0 reduce-scatter.2.cloned.1.call-update
  492.6 175.1 %reduce-scatter.2.cloned.1.call-done = bf16[256,12544]{0,1:T(8,128)(2,1)} async-done(((bf16[1024,12544]{0,1:T(8,128)(2,1)}), bf16[256,12544]{0,1:T(8,128)(2,1)}) %reduce-scatter.2.cloned.1.call-update) | async-done | bytes 6422544 | tf_op jit(solution)/shard_map/reduce_scatter | solution.py:46
  667.7 0.0 copy-done
  667.7 0.0 copy-done.1
  667.7 0.0 copy-done.2
  667.7 15.5 %fusion.14 = bf16[256,1024]{1,0:T(8,128)(2,1)} fusion(bf16[1024,1024]{1,0:T(8,128)(2,1)S(1)} %copy-done, bf16[256,12544]{0,1:T(8,128)(2,1)} %reduce-scatter.2.cloned.1.call-done, bf16[12544,1024]{1,0:T(8,128)(2,1)} %param.8, f32[1024]{0:T(1024)S(1)} %copy-done.2, f32[1024]{0:T(1024)S(1)} %copy-done.1), kind=kOutput, calls=%fused_computation.20 | convolution fusion | flops 7115112448 | bytes 34742272 | tf_op jit(solution)/shard_map/dot_general | solution.py:29
  (2 shorter events, 0.0 us)
Async XLA Ops:
  6.5 661.1 %copy-start = (bf16[1024,1024]{1,0:T(8,128)(2,1)S(1)}, bf16[1024,1024]{1,0:T(8,128)(2,1)}, u32[]{:S(2)}) copy-start(bf16[1024,1024]{1,0:T(8,128)(2,1)} %param.10) | copy-start | bytes 6291460
  6.5 661.1 %reduce-scatter.2.cloned.1.call-start = ((), (), s32[]{:S(2)}) async-start(), calls=%async_computation.1 | async-start | bytes 32112640 | tf_op jit(solution)/shard_map/reduce_scatter | solution.py:46
  492.5 175.2 %copy-start.1 = (f32[1024]{0:T(1024)S(1)}, f32[1024]{0:T(1024)}, u32[]{:S(2)}) copy-start(f32[1024]{0:T(1024)} %param.9) | copy-start | bytes 12292
  492.5 175.2 %copy-start.2 = (f32[1024]{0:T(1024)S(1)}, f32[1024]{0:T(1024)}, u32[]{:S(2)}) copy-start(f32[1024]{0:T(1024)} %param.11) | copy-start | bytes 12292
Sparse Core Ops, SparseCore 0:
  492.7 174.9 reduce-scatter.1
where the time goes:
time: 691 us; the launch traced here: 690 us
  matrix products  443 us (64%)
  waiting for transfers between devices  175 us (25%)
  local copies, waits for them, and re-layouts  41.3 us (6%)
  other arithmetic  17.1 us (2%)
  between operations  13.4 us (2%)
    dot_general x1, matrix products, device_step(): jnp.einsum('rih,rjhc->rijc', row_wts.astype(jnp.float32), across, precisi...  298 us
    reduce_scatter x1, waiting for transfers between devices, device_step(): pooled = lax.psum_scatter(tile_part, 'sp', scatter_dimension=0, tiled=True)  175 us
    dot_general x1, matrix products, device_step(): jnp.einsum('rjw,hwc->rjhc', col_wts, feature_map, preferred_element_type=...  130 us
    convert_element_type x1, local copies, waits for them, and re-layouts, device_step(): tile_part.astype(jnp.bfloat16)  38.6 us
    dot_general x1, matrix products, box_head(): jnp.dot(hidden_act, w_two, preferred_element_type=jnp.float32) + b_two  15.5 us
    reduce_sum x2, other arithmetic, bin_weights(): weights.reshape(weights.shape[:-2] + (POOL_BINS, 2, num_rows)).sum(axis=-2)  15.3 us
  transfers between devices with their start and end apart: 1, of which 1 were waited for; matrix products, arithmetic and copies ran while one was open for 0% of the time, Pallas kernels for 0%

commit v1 on v0

v1 whole, which is shorter than its diff:
```python
import functools

import jax
import jax.numpy as jnp
from jax import lax
from jax.experimental import pallas as pl
from jax.experimental.pallas import tpu as pltpu
from jax.sharding import PartitionSpec as P

BINS = 7
SAMPLES = 2 * BINS
HALO = 6
WINDOW = 256
BLOCK = 16
SLOTS = 11


def sample_rows(start_eighths, span_units, length):
    ids = jnp.arange(SAMPLES, dtype=jnp.int32)
    pos = 4 * start_eighths[..., None] - 16 + (2 * ids + 1) * span_units[..., None]
    inside = (pos >= -32) & (pos <= 32 * length)
    return pos, inside


def column_table(boxes, feat_w):
    pos, inside = sample_rows(boxes[..., 1], (boxes[..., 3] - boxes[..., 1]) // 7, feat_w)
    pos = jnp.clip(pos, 0, 32 * (feat_w - 1))
    right = pos[..., 0] // 32 >= feat_w - WINDOW
    shift = jnp.where(right, feat_w - WINDOW, 0)
    at = (pos - 32 * shift[..., None]).astype(jnp.float32) / 32.0
    gain = jnp.where(inside, 0.5, 0.0)
    pad = [(0, 0)] * (at.ndim - 1) + [(0, 1)]
    cols = lax.broadcasted_iota(jnp.float32, at.shape[:-1] + (BINS + 1, WINDOW), at.ndim)

    def tent(which):
        x = jnp.pad(at[..., which::2], pad)[..., None]
        g = jnp.pad(gain[..., which::2], pad)[..., None]
        return jnp.maximum(1.0 - jnp.abs(cols - x), 0.0) * g

    return tent(0) + tent(1), right


def row_lists(boxes, right, chip, tile_rows, length):
    regions = boxes.shape[-2]
    chip_rows = 2 * tile_rows
    lists = chip_rows + HALO - 1
    width = regions + 2 * BLOCK
    pos, inside = sample_rows(boxes[..., 0], (boxes[..., 2] - boxes[..., 0]) // 7, length)
    pos = jnp.maximum(pos, 0)
    at_top = pos // 32 >= length - 1
    low = jnp.where(at_top, length - 2, pos // 32)
    frac = jnp.where(at_top, 32, pos % 32)
    first, last = low[..., 0::2], low[..., 1::2] + 1
    owned = (first + last) // 2 // chip_rows == chip
    tile = first // tile_rows
    straddle = owned & (last // tile_rows > tile)
    edge = (tile + 1) * tile_rows
    parity = tile % 2

    def per_sample(a):
        return jnp.repeat(a, 2, axis=-1)

    ids = jnp.arange(regions, dtype=jnp.int32)[:, None]
    bin_slot = 1 + jnp.arange(SAMPLES, dtype=jnp.int32) // 2
    part_slot = 1 + BINS + per_sample(parity)
    upper = per_sample(straddle) & (low >= per_sample(edge))
    split = per_sample(straddle) & (low == per_sample(edge) - 1)
    live = per_sample(owned) & inside
    start = chip * (chip_rows - HALO)
    head = frac + (ids << 18)
    code_one = head + ((ids * SLOTS + jnp.where(upper, part_slot, bin_slot)) << 6)
    code_two = head + ((ids * SLOTS + part_slot) << 6)
    list_one = jnp.where(live, low - start, -1)
    list_two = jnp.where(live & split, lists + per_sample(tile) - chip, -1)
    list_ids = jnp.arange(lists + 2, dtype=jnp.int32)[:, None]
    lo = jnp.moveaxis(list_one, -1, 0)[..., None, :]
    hi = jnp.moveaxis(list_two, -1, 0)[..., None, :]
    co = jnp.moveaxis(code_one, -1, 0)[..., None, :]
    ch = jnp.moveaxis(code_two, -1, 0)[..., None, :]
    code = jnp.sum(jnp.where(lo == list_ids, co, 0) + jnp.where(hi == list_ids, ch, 0), axis=0)
    touch = jnp.sum((lo == list_ids).astype(jnp.int32) + (hi == list_ids).astype(jnp.int32), axis=0) > 0

    is_right = right[..., None, :]
    kinds = jnp.stack([touch & ~is_right, touch & is_right])
    before = (jnp.arange(regions)[:, None] < jnp.arange(regions)[None, :]).astype(jnp.bfloat16)
    rank = jnp.einsum('tgvr,rs->tgvs', kinds.astype(jnp.bfloat16), before, preferred_element_type=jnp.float32).astype(jnp.int32)
    place = jnp.where(is_right, width - 1 - rank[1], rank[0])
    place = jnp.where(touch, place, -1)
    count = jnp.sum(kinds.astype(jnp.int32), axis=-1)
    seats = jnp.arange(width, dtype=jnp.int32)
    table = jnp.sum(jnp.where(place[..., :, None] == seats, code[..., :, None], 0), axis=-2)
    table = jnp.pad(table, ((0, 0), (0, 1), (0, 0)))

    blocks = (jnp.moveaxis(count, 0, -1).reshape(count.shape[1], -1) + BLOCK - 1) // BLOCK
    order = jnp.arange(blocks.shape[-1], dtype=jnp.int32)
    upto = jnp.sum(jnp.where(order[:, None] <= order[None, :], blocks[:, :, None], 0), axis=1)
    total = upto[:, -1]
    most = (regions * (SAMPLES + 2) + (BLOCK - 1) * blocks.shape[-1]) // BLOCK + 4
    turn = jnp.arange(most, dtype=jnp.int32) - 1
    which = jnp.sum((upto[:, None, :] <= turn[:, None]).astype(jnp.int32), axis=-1)
    nth = turn - jnp.sum(jnp.where(order < which[..., None], blocks[:, None, :], 0), axis=-1)
    kind = which % 2
    base = jnp.where(kind == 1, width - BLOCK * (nth + 1), BLOCK * nth)
    real = (turn >= 0) & (turn < total[:, None])
    plan = jnp.where(real, which // 2 + (kind << 8) + (base << 9), lists + 2)

    edges = (jnp.arange(2, dtype=jnp.int32) + 1 + chip) * tile_rows - 1 - start
    every = jnp.arange(lists, dtype=jnp.int32)
    row_of = jnp.concatenate([every, edges, jnp.zeros((1,), jnp.int32)])
    on_edge = (every == edges[0]) | (every == edges[1])
    low_gain = jnp.concatenate([jnp.full((lists,), 1 / 64), jnp.zeros((3,))]).astype(jnp.float32)
    high_gain = jnp.concatenate([jnp.where(on_edge, 0.0, 1 / 64), jnp.full((2,), 1 / 64), jnp.zeros((1,))]).astype(jnp.float32)

    bins = jnp.arange(BINS, dtype=jnp.int32) + 1
    joins = jnp.stack([jnp.sum(jnp.where(straddle & (parity == q), bins, 0), axis=-1) for q in range(2)], axis=-1)
    return table.reshape(table.shape[0], -1), plan, total, row_of, low_gain, high_gain, joins.reshape(joins.shape[0], -1)


def pool_kernel(dims, list_ref, plan_ref, meta_ref, row_ref, low_ref, high_ref, join_ref, tab_ref, own_ref, mate_ref, halo_ref, w_ref, out_ref,
                feat, acc_a, acc_b, lhs, wbuf, out_one, out_two, fsem, wsem):
    tile_rows, feat_w, channels, regions, width = dims
    chip, core, total = meta_ref[0], meta_ref[1], meta_ref[2]
    half = channels // 2
    row_in = BINS * channels
    first = chip * HALO
    copies = [
        pltpu.make_async_copy(own_ref, feat.at[pl.ds(first + core * tile_rows, tile_rows)], fsem.at[0]),
        pltpu.make_async_copy(mate_ref, feat.at[pl.ds(first + (1 - core) * tile_rows, tile_rows)], fsem.at[1]),
        pltpu.make_async_copy(halo_ref, feat.at[pl.ds((1 - chip) * 2 * tile_rows, HALO)], fsem.at[2]),
    ]
    for copy in copies:
        copy.start()
    depth = wbuf.shape[0]

    def weights(i):
        return pltpu.make_async_copy(w_ref.at[pl.ds(i * row_in, row_in)], wbuf.at[i % depth], wsem.at[i % depth])

    for i in range(depth):
        weights(i).start()

    zero = jnp.zeros((8 * SLOTS, half), jnp.float32)

    def clear(r, _):
        at = pl.ds(pl.multiple_of(r * 8 * SLOTS, 8), 8 * SLOTS)
        acc_a[at, :] = zero
        acc_b[at, :] = zero
        return 0

    lax.fori_loop(0, regions, clear, 0)
    for copy in copies:
        copy.wait()

    def multiply(turn, out):
        plan = plan_ref[turn]
        v = plan & 255
        column = pl.multiple_of(((plan >> 8) & 1) * (feat_w - WINDOW), 16)
        at = v * width + (plan >> 9)
        rows = [tab_ref[list_ref[at + s] >> 18] for s in range(BLOCK)]
        left = jnp.concatenate(rows, axis=0).astype(jnp.bfloat16)
        row = row_ref[v]
        out[0] = jnp.dot(left, feat[row, pl.ds(column, WINDOW), :], preferred_element_type=jnp.float32)
        out[1] = jnp.dot(left, feat[row + 1, pl.ds(column, WINDOW), :], preferred_element_type=jnp.float32)

    def spread(turn, out):
        plan = plan_ref[turn]
        v = plan & 255
        at = v * width + (plan >> 9)
        low, high = low_ref[v], high_ref[v]
        for s0 in range(0, BLOCK, 4):
            slots, news = [], []
            for s in range(s0, s0 + 4):
                code = list_ref[at + s]
                frac = (code & 63).astype(jnp.float32)
                wl, wh = (32.0 - frac) * low, frac * high
                slot = pl.ds(pl.multiple_of(((code >> 6) & 4095) * 8, 8), 8)
                slots.append(slot)
                news.append((
                    acc_a[slot, :] + (out[0, 8 * s:8 * s + 8, :half] * wl + out[1, 8 * s:8 * s + 8, :half] * wh),
                    acc_b[slot, :] + (out[0, 8 * s:8 * s + 8, half:] * wl + out[1, 8 * s:8 * s + 8, half:] * wh),
                ))
            for slot, (a, b) in zip(slots, news):
                acc_a[slot, :] = a
                acc_b[slot, :] = b

    def pair(u, _):
        multiply(2 * u + 1, out_one)
        spread(2 * u, out_two)
        multiply(2 * u + 2, out_two)
        spread(2 * u + 1, out_one)
        return 0

    pairs = (total + 1) // 2
    out_two[...] = jnp.zeros_like(out_two)
    lax.fori_loop(0, pairs, pair, 0)
    spread(2 * pairs, out_two)

    def join(r, _):
        for q in range(2):
            to = pl.ds(pl.multiple_of((r * SLOTS + join_ref[2 * r + q]) * 8, 8), 8)
            part = pl.ds(pl.multiple_of((r * SLOTS + 1 + BINS + q) * 8, 8), 8)
            for acc in (acc_a, acc_b):
                acc[to, :] = acc[to, :].astype(jnp.bfloat16).astype(jnp.float32) + acc[part, :].astype(jnp.bfloat16).astype(jnp.float32)
        return 0

    lax.fori_loop(0, regions, join, 0)

    for i in range(BINS):
        for j in range(BINS):
            rows = pl.ds((1 + i) * 8 + j, regions, stride=8 * SLOTS)
            lhs[i % 2, :, j * channels:j * channels + half] = acc_a[rows, :].astype(jnp.bfloat16)
            lhs[i % 2, :, j * channels + half:(j + 1) * channels] = acc_b[rows, :].astype(jnp.bfloat16)
        weights(i).wait()
        part = jnp.dot(lhs[i % 2], wbuf[i % depth], preferred_element_type=jnp.float32)
        if i == 0:
            out_ref[...] = part
        else:
            out_ref[...] += part
        if i + depth < BINS:
            weights(i + depth).start()


def pool_and_project(lists, plan, meta, row_of, low_gain, high_gain, joins, tab, own, mate, halo, w_one):
    tile_rows, feat_w, channels = own.shape
    regions = tab.shape[0]
    hidden = w_one.shape[1]
    row_in = BINS * channels
    depth = 3
    dims = (tile_rows, feat_w, channels, regions, regions + 2 * BLOCK)
    smem = pl.BlockSpec(memory_space=pltpu.SMEM)
    vmem = pl.BlockSpec(memory_space=pltpu.VMEM)
    hbm = pl.BlockSpec(memory_space=pl.ANY)
    return pl.pallas_call(
        functools.partial(pool_kernel, dims),
        out_shape=jax.ShapeDtypeStruct((regions, hidden), jnp.float32),
        in_specs=[smem] * 7 + [vmem] + [hbm] * 4,
        out_specs=vmem,
        scratch_shapes=[
            pltpu.VMEM((2 * tile_rows + HALO, feat_w, channels), jnp.bfloat16),
            pltpu.VMEM((regions * SLOTS * 8, channels // 2), jnp.float32),
            pltpu.VMEM((regions * SLOTS * 8, channels // 2), jnp.float32),
            pltpu.VMEM((2, regions, row_in), jnp.bfloat16),
            pltpu.VMEM((depth, row_in, hidden), jnp.bfloat16),
            pltpu.VMEM((2, BLOCK * 8, channels), jnp.float32),
            pltpu.VMEM((2, BLOCK * 8, channels), jnp.float32),
            pltpu.SemaphoreType.DMA((3,)),
            pltpu.SemaphoreType.DMA((depth,)),
        ],
        compiler_params=pltpu.CompilerParams(vmem_limit_bytes=64 * 1024 * 1024 - 65536),
        cost_estimate=pl.CostEstimate(flops=30_000_000_000, bytes_accessed=50_000_000, transcendentals=0),
        name='pool',
    )(lists, plan, meta, row_of, low_gain, high_gain, joins, tab, own, mate, halo, w_one)


def solution(mesh):
    group = mesh.shape['sp']

    def device_step(feature_map, box_coords, w_one, b_one, w_two, b_two):
        tile_rows, feat_w, channels = feature_map.shape
        regions = box_coords.shape[0] // group
        me = lax.axis_index('sp')
        chip, core = me // 2, me % 2

        mate = lax.ppermute(feature_map, 'sp', [(0, 1), (1, 0), (2, 3), (3, 2)])
        rim = jnp.where(core == 1, feature_map[tile_rows - HALO:], feature_map[:HALO])
        hop_one = lax.ppermute(rim, 'sp', [(1, 2), (2, 1)])
        hop_two = lax.ppermute(hop_one, 'sp', [(1, 0), (2, 3)])
        halo = jnp.where((me == 1) | (me == 2), hop_one, hop_two)

        far = (me + 2) % 4
        boxes = jnp.stack([lax.dynamic_slice_in_dim(box_coords, g * regions, regions, 0) for g in (far, me)])
        tab, right = column_table(boxes, feat_w)
        lists, plan, total, row_of, low_gain, high_gain, joins = row_lists(boxes, right, chip, tile_rows, tile_rows * group)

        def project(g):
            meta = jnp.stack([chip, core, total[g]])
            return pool_and_project(lists[g], plan[g], meta, row_of, low_gain, high_gain, joins[g], tab[g], feature_map, mate, halo, w_one)

        away = project(0)
        back = lax.ppermute(away, 'sp', [(0, 2), (2, 0), (1, 3), (3, 1)])
        here = project(1)
        hidden_act = jnp.maximum(here + back + b_one, 0.0).astype(jnp.bfloat16)
        return jnp.maximum(jnp.dot(hidden_act, w_two, preferred_element_type=jnp.float32) + b_two, 0.0).astype(jnp.bfloat16)

    return jax.shard_map(device_step, mesh=mesh, in_specs=(P(('dp', 'sp'), None, None), P('dp', None), P(), P(), P(), P()), out_specs=P(('dp', 'sp'), None), check_vma=False)
```

time: 691 us -> 183 us (0.26)
  the two profiles are of different devices: /device:TPU:0 before, /device:TPU:2 now
where the time goes in v1:
time: 183 us; the launch traced here: 182 us
  Pallas kernels  116 us (63%)
  other arithmetic  43.4 us (24%)
  local copies, waits for them, and re-layouts  14.6 us (8%)
  matrix products  3.92 us (2%)
  starting transfers between devices  3.3 us (2%)
    pallas_call x2, Pallas kernels, pool_and_project(): pl.pallas_call(functools.partial(pool_kernel, dims), out_shape=jax.ShapeD...  116 us
    reduce_sum x1, other arithmetic, row_lists(): jnp.sum(jnp.where(place[..., :, None] == seats, code[..., :, None], 0), a...  23.7 us
    reduce_sum x1, other arithmetic, row_lists(): jnp.sum((lo == list_ids).astype(jnp.int32) + (hi == list_ids).astype(jnp....  6.46 us
    dot_general x1, matrix products, device_step(): jnp.dot(hidden_act, w_two, preferred_element_type=jnp.float32) + b_two  3.69 us
  transfers between devices with their start and end apart: 4, of which 0 were waited for; matrix products, arithmetic and copies ran while one was open for 32% of the time, Pallas kernels for 32%

profile of v1, /device:TPU:2, one launch (start us, length us, event | category | flops | bytes accessed | tf_op | source)
XLA Modules:
  0.0 182.0 jit_solution(380846475019087509)
XLA Ops:
  0.0 1.6 slice_select_fusion
  1.6 1.9 %collective-permute-start.1 = (bf16[6,336,256]{2,1,0:T(8,128)(2,1)S(1)}, bf16[6,336,256]{2,1,0:T(8,128)(2,1)S(1)}, u32[]{:S(2)}, u32[]{:S(2)}) collective-permute-start(bf16[6,336,256]{2,1,0:T(8,128)(2,1)S(1)} %slice_select_fusion), channel_id=1, source_target_pairs={{1,2},{2,1},{5,6},{6,5}} | collective-permute-start | bytes 3096584 | tf_op jit(solution)/shard_map/ppermute | solution.py:265
  3.6 0.7 dynamic-slice_bitcast_fusion.1
  5.5 0.7 squeeze.52.join_ref
  6.4 0.7 squeeze.48.join_ref
  7.9 6.5 %add_reduce_fusion.1 = (s32[2,107,256]{2,0,1:T(2,128)S(1)}, s32[2,107,256]{2,0,1:T(2,128)}) fusion(s32[14,2,256]{2,1,0:T(2,128)S(1)} %copy.97, s32[14,2,256]{2,1,0:T(2,128)S(1)} %copy.92, s32[14,2,256]{2,1,0:T(2,128)S(1)} %copy.104, s32[14,2,256]{2,1,0:T(2,128)S(1)} %copy.102), kind=kLoop, calls=%fused_computation.4 | loop fusion | flops 7560192 | bytes 552960 | tf_op jit(solution)/shard_map/reduce_sum | solution.py:81
  14.6 0.8 copy.106
  15.4 1.0 sub.208
  16.6 0.4 select_reduce_fusion.1
  17.0 0.8 copy.108
  17.8 0.9 copy.105
  19.1 23.7 %select_reduce_fusion = s32[2,107,288]{2,1,0:T(8,128)S(1)} fusion(s32[2,107,256]{2,1,0:T(8,128)S(1)} %copy.105, s32[2,107,256]{2,1,0:T(8,128)S(1)} %fusion.9), kind=kLoop, calls=%fused_computation | loop fusion | flops 47271744 | bytes 684800 | tf_op jit(solution)/shard_map/reduce_sum | solution.py:91
  42.8 0.7 pad_slice_fusion
  43.5 1.7 squeeze.50.list_ref
  45.2 0.8 squeeze.44.list_ref
  46.0 0.6 fusion.68
  46.6 1.2 pad_add_fusion.7.meta_ref
  47.8 1.2 pad_add_fusion.4.meta_ref
  49.0 0.6 pad_add_fusion.6.row_ref
  49.6 0.6 fusion.69
  50.2 1.2 or_select_fusion
  51.6 1.5 fusion.2
  53.0 0.6 fusion.3
  53.7 0.5 fusion.67
  54.2 1.3 collective-permute-start.2
  55.6 0.6 pad_maximum_fusion.high_ref
  56.2 2.3 %multiply_add_fusion = f32[2,256,8,256]{3,2,1,0:T(8,128)S(1)} fusion(f32[2,256,8]{2,1,0:T(8,128)S(1)} %pad.22.clone, f32[2,256,8]{2,1,0:T(8,128)S(1)} %pad.21.clone, f32[2,256,8]{2,1,0:T(8,128)S(1)} %pad.20.clone, f32[2,256,8]{2,1,0:T(8,128)S(1)} %pad.19.clone), kind=kLoop, calls=%fused_computation.2 | loop fusion | flops 11534336 | bytes 4259840 | tf_op jit(solution)/shard_map/add | solution.py:40
  58.5 2.3 %slice_bitcast_fusion = (f32[256,8,256]{2,1,0:T(8,128)}, f32[256,8,256]{2,1,0:T(8,128)}) fusion(f32[2,256,8,256]{3,2,1,0:T(8,128)S(1)} %multiply_add_fusion), kind=kLoop, calls=%fused_computation.7 | loop fusion | bytes 8388608 | tf_op jit(solution)/shard_map/squeeze | solution.py:276
  60.8 1.1 broadcast_select_fusion.halo_ref
  61.9 58.2 %pool.3 = f32[256,1024]{1,0:T(8,128)} custom-call(s32[31104]{0:T(1024)} %squeeze.50.list_ref, s32[460]{0:T(512)} %bitcast.83, s32[3]{0:T(128)} %pad_add_fusion.7.meta_ref, s32[108]{0:T(128)} %pad_add_fusion.6.row_ref, f32[108]{0:T(128)} %constant.244.clone.1.low_ref, f32[108]{0:T(128)} %pad_maximum_fusion.high_ref, s32[512]{0:T(512)} %squeeze.52.join_ref, ...), custom_call_target="tpu_custom_call" | custom-call | flops 30000001024 | bytes 50000000 | tf_op jit(solution)/shard_map/pool/pallas_call | solution.py:232
  120.1 58.1 %pool.2 = f32[256,1024]{1,0:T(8,128)} custom-call(s32[31104]{0:T(1024)} %squeeze.44.list_ref, s32[460]{0:T(512)} %bitcast.82, s32[3]{0:T(128)} %pad_add_fusion.4.meta_ref, s32[108]{0:T(128)} %pad_add_fusion.6.row_ref, f32[108]{0:T(128)} %constant.244.clone.1.low_ref, f32[108]{0:T(128)} %pad_maximum_fusion.high_ref, s32[512]{0:T(512)} %squeeze.48.join_ref, ...), custom_call_target="tpu_custom_call" | custom-call | flops 30000001024 | bytes 50000000 | tf_op jit(solution)/shard_map/pool/pallas_call | solution.py:232
  178.3 3.7 %fusion.1 = bf16[256,1024]{1,0:T(8,128)(2,1)} fusion(bf16[1024,1024]{1,0:T(8,128)(2,1)} %param.10, f32[256,1024]{1,0:T(8,128)} %pool.2, f32[256,1024]{1,0:T(8,128)} %collective-permute-done.3, f32[1024]{0:T(1024)} %param.11, f32[1024]{0:T(1024)} %param.9), kind=kOutput, calls=%fused_computation.13 | convolution fusion | flops 538705920 | bytes 4726784 | tf_op jit(solution)/shard_map/dot_general | solution.py:282
  (67 shorter events, 2.8 us)
Async XLA Ops:
  0.0 61.9 %collective-permute-start = (bf16[50,336,256]{2,1,0:T(8,128)(2,1)}, bf16[50,336,256]{2,1,0:T(8,128)(2,1)}, u32[]{:S(2)}, u32[]{:S(2)}) collective-permute-start(bf16[50,336,256]{2,1,0:T(8,128)(2,1)} %own_ref.3), channel_id=1, source_target_pairs={{0,1},{1,0},{2,3},{3,2},{4,5},{5,4},{6,7},{7,6}} | collective-permute-start | bytes 25804808 | tf_op jit(solution)/shard_map/ppermute | solution.py:263
  1.6 52.6 %collective-permute-start.1 = (bf16[6,336,256]{2,1,0:T(8,128)(2,1)S(1)}, bf16[6,336,256]{2,1,0:T(8,128)(2,1)S(1)}, u32[]{:S(2)}, u32[]{:S(2)}) collective-permute-start(bf16[6,336,256]{2,1,0:T(8,128)(2,1)S(1)} %slice_select_fusion), channel_id=1, source_target_pairs={{1,2},{2,1},{5,6},{6,5}} | collective-permute-start | bytes 3096584 | tf_op jit(solution)/shard_map/ppermute | solution.py:265
  54.2 6.6 %collective-permute-start.2 = (bf16[6,336,256]{2,1,0:T(8,128)(2,1)S(1)}, bf16[6,336,256]{2,1,0:T(8,128)(2,1)S(1)}, u32[]{:S(2)}, u32[]{:S(2)}) collective-permute-start(bf16[6,336,256]{2,1,0:T(8,128)(2,1)S(1)} %collective-permute-done.1), channel_id=1, source_target_pairs={{1,0},{2,3},{5,4},{6,7}} | collective-permute-start | bytes 3096584 | tf_op jit(solution)/shard_map/ppermute | solution.py:266
  120.1 58.2 %collective-permute-start.3 = (f32[256,1024]{1,0:T(8,128)}, f32[256,1024]{1,0:T(8,128)}, u32[]{:S(2)}, u32[]{:S(2)}) collective-permute-start(f32[256,1024]{1,0:T(8,128)} %pool.3), channel_id=1, source_target_pairs={{0,2},{2,0},{1,3},{3,1},{4,6},{6,4},{5,7},{7,5}} | collective-permute-start | bytes 3145736 | tf_op jit(solution)/shard_map/ppermute | solution.py:279
